TPU v7x, 32 devices: a whole 2x2x4 slice. The times are simulated.
32 devices in a mesh: dp: 8 (over z, y), neg: 4 (over x, core).
Axes of the slice: x: 2, y: 2, z: 4, core: 2. Of those that a mesh axis runs over, the one named last changes fastest.
Arguments:
- user_embed: bfloat16 [24576, 256], P(('dp', 'neg')), may hold values from -25 to 25
- positive_embed: bfloat16 [24576, 256], P(('dp', 'neg')), may hold values from -6 to 6
- positive_ids: int32 [24576], P(('dp', 'neg')), may hold values from 0 to 1048575
- token_weights: int32 [24576], P(('dp', 'neg')), may hold values from 1 to 5
- offsets: int32 [8, 25], P('dp'), may hold values from 0 to 3072, as said below
- negative_embed: bfloat16 [32768, 256], P('neg'), may hold values from -6 to 6
- negative_ids: int32 [32768], P('neg'), may hold values from 0 to 1048575
Outputs:
- token_loss: float32 [24576], P(('dp', 'neg'))
- mean_loss: float32 [], replicated
Inputs may be any that keep to these rules, and one draw needn't show every extreme that they name: `offsets`: each row starts at 0 and does not fall; every user holds 2 or more slots; in every draw some group fills all 3072 slots.
All inputs are finite; a program needn't handle non-finite values.
Results may differ from a plain program's by a relative error of at most 0.0003.
Values may be sent and summed in bfloat16 or wider, within the bound.
No kernel may reach another device: no remote copies, remote signals or barrier semaphores. Data moves between devices by JAX's collectives and lax.ppermute only.
A program may use at most 64 MiB of HBM per device.

v0:
```python
import math
import jax
import jax.numpy as jnp
from jax import lax
from jax.sharding import PartitionSpec as P

floor_value = -1e30


def merged(value, axis, join):
    pieces = jax.tree.map(lambda part: lax.all_gather(part, axis), value)
    head = jax.tree.map(lambda part: part[0], pieces)
    tail = jax.tree.map(lambda part: part[1:], pieces)
    total, _ = lax.scan(lambda total, share: (join(total, share), None), head, tail)
    return total


def shard_partials(rows, row_ids, columns, column_ids, scale):
    logits = (
        lax.dot_general(rows, columns, (((1,), (1,)), ((), ())), preferred_element_type=jnp.float32)
        * scale
    )
    hit = row_ids[:, None] == column_ids[None, :]
    peak = jnp.max(jnp.where(hit, floor_value, logits), axis=1)
    summed = jnp.sum(jnp.where(hit, 0.0, jnp.exp(logits - peak[:, None])), axis=1)
    return (peak, summed)


def combine(first, second):
    peak = jnp.maximum(first[0], second[0])
    return (peak, first[1] * jnp.exp(first[0] - peak) + second[1] * jnp.exp(second[0] - peak))


def shards(
    user_embed, positive_embed, positive_ids, token_weights, offsets, negative_embed, negative_ids
):
    tok_rows = user_embed.shape[0]
    width = user_embed.shape[1]
    scale = 3.0 / math.sqrt(width)
    positions = lax.axis_index("neg") * tok_rows + jnp.arange(tok_rows, dtype=jnp.int32)
    ends = offsets[0, 1:]
    last_slot = jnp.any(positions[:, None] + 1 == ends[None, :], axis=1)
    live = (positions < offsets[0, -1]) & jnp.logical_not(last_slot)
    weight = token_weights.astype(jnp.float32)
    live_weight = weight * live.astype(jnp.float32)
    rows = lax.all_gather(user_embed, "neg", axis=0, tiled=True)
    row_ids = lax.all_gather(positive_ids, "neg", axis=0, tiled=True)
    number = rows.shape[0]
    block = math.gcd(number, 512)
    blocks = rows.reshape(number // block, block, width)
    id_blocks = row_ids.reshape(number // block, block)

    def one_block(pair):
        return shard_partials(pair[0], pair[1], negative_embed, negative_ids, scale)

    peaks, sums = lax.map(one_block, (blocks, id_blocks))
    new_peaks = peaks.reshape(number)
    new_sums = sums.reshape(number)
    peaks = new_peaks
    sums = new_sums
    peaks, sums = merged((peaks, sums), "neg", combine)
    own_start = lax.axis_index("neg") * tok_rows
    peaks = lax.dynamic_slice_in_dim(peaks, own_start, tok_rows, 0)
    sums = lax.dynamic_slice_in_dim(sums, own_start, tok_rows, 0)
    positive = (
        jnp.sum(user_embed.astype(jnp.float32) * positive_embed.astype(jnp.float32), axis=1) * scale
    )
    top = jnp.maximum(peaks, positive)
    lse = top + jnp.log(sums * jnp.exp(peaks - top) + jnp.exp(positive - top))
    token_loss = jnp.where(live, lse - positive, 0.0).astype(jnp.float32)
    weighted = jnp.sum(weight * token_loss)
    total, count = lax.psum((weighted, jnp.sum(live_weight)), ("dp", "neg"))
    return (token_loss, total / count)


def solution(mesh):
    in_specs = (
        P(("dp", "neg"), None),
        P(("dp", "neg"), None),
        P(("dp", "neg")),
        P(("dp", "neg")),
        P("dp", None),
        P("neg", None),
        P("neg"),
    )
    out_specs = (P(("dp", "neg")), P())
    return jax.shard_map(shards, mesh=mesh, in_specs=in_specs, out_specs=out_specs, check_vma=False)
```

profile of v0, /device:TPU:0, one launch (start us, length us, event | category | flops | bytes accessed | tf_op | source)
XLA Modules:
  0.0 153.4 jit_solution(13548246562837746475)
XLA Ops:
  7.2 0.0 all-gather.5.cloned.1.call-start
  7.2 0.7 all-gather.5.cloned.1.call-update
  7.9 0.7 reshape.22
  8.6 6.2 %all-gather = s32[4,1,768]{2,1,0:T(1,128)S(1)} all-gather(s32[1,1,768]{2,1,0:T(1,128)S(1)} %reshape.22), channel_id=1, replica_groups=mesh['dp'=8,'neg'=4] {'neg'}, dimensions={0}, use_global_device_ids=true | all-gather | bytes 15360 | tf_op jit(solution)/shard_map/all_gather | solution.py:47
  14.9 1.2 slice.18
  16.1 0.7 slice_bitcast_fusion
  16.8 0.1 compare_reduce_fusion
  16.9 1.3 multiply_reduce_fusion
  18.2 13.7 %all-gather.5.cloned.1.call-done = bf16[3072,256]{1,0:T(8,128)(2,1)} async-done(((bf16[768,256]{1,0:T(8,128)(2,1)}), bf16[3072,256]{1,0:T(8,128)(2,1)}) %all-gather.5.cloned.1.call-update) | async-done | bytes 1572880 | tf_op jit(solution)/shard_map/all_gather | solution.py:46
  31.9 0.0 copy-start.1
  31.9 59.9 %while.24 = (s32[]{:T(128)}, f32[6,512]{1,0:T(8,128)S(1)}, f32[6,512]{1,0:T(8,128)S(1)}, s32[6,512]{1,0:T(8,128)S(1)}, s32[8192]{0:T(1024)}, /*index=5*/bf16[6,5...) while((s32[]{:T(128)}, f32[6,512]{1,0:T(8,128)S(1)}, f32[6,512]{1,0:T(8,128)S(1)}, ...), condition=%wide.region_4.5_spmd, body=%wide.region_1.4_spmd.sunk | while | flops 2185231360 | bytes 38230660 | solution.py:56
  31.9 0.0 copy-start
  31.9 5.1 %fusion.16 = (f32[512]{0:T(512)S(1)}, f32[512,8192]{1,0:T(8,128)S(1)}) fusion(s32[8192]{0:T(1024)} %get-tuple-element.215, s32[512]{0:T(512)S(1)} %bitcast.44, bf16[8192,256]{1,0:T(8,128)(2,1)} %get-tuple-element.217, bf16[6,512,256]{2,1,0:T(8,128)(2,1)} %get-tuple-element.216, s32[]{:T(128)} %get-tuple-element.202), kind=kOutput, calls=%fused_computation.2.clone.1 | convolution fusion | flops 2164260352 | bytes 21271040 | tf_op jit(solution)/shard_map/while/body/eval_jaxpr/dot_general | solution.py:20
  37.1 0.0 copy-done
  37.1 4.6 %fusion.17 = f32[512]{0:T(512)S(1)} fusion(f32[512,8192]{1,0:T(8,128)S(1)} %get-tuple-element.183, f32[512]{0:T(512)S(1)} %get-tuple-element.182, s32[8192]{0:T(1024)S(1)} %copy-done, s32[512]{0:T(512)S(1)} %bitcast.45), kind=kLoop, calls=%fused_computation.3.clone.1 | loop fusion | flops 20971008 | bytes 16816128 | tf_op jit(solution)/shard_map/while/body/eval_jaxpr/reduce_sum | solution.py:25
  41.7 0.1 dynamic_update_slice.10
  41.8 0.1 dynamic_update_slice.9
  41.9 0.0 copy-start
  41.9 5.1 %fusion.16 = (f32[512]{0:T(512)S(1)}, f32[512,8192]{1,0:T(8,128)S(1)}) fusion(s32[8192]{0:T(1024)} %get-tuple-element.215, s32[512]{0:T(512)S(1)} %bitcast.44, bf16[8192,256]{1,0:T(8,128)(2,1)} %get-tuple-element.217, bf16[6,512,256]{2,1,0:T(8,128)(2,1)} %get-tuple-element.216, s32[]{:T(128)} %get-tuple-element.202), kind=kOutput, calls=%fused_computation.2.clone.1 | convolution fusion | flops 2164260352 | bytes 21271040 | tf_op jit(solution)/shard_map/while/body/eval_jaxpr/dot_general | solution.py:20
  47.1 0.0 copy-done
  47.1 4.6 %fusion.17 = f32[512]{0:T(512)S(1)} fusion(f32[512,8192]{1,0:T(8,128)S(1)} %get-tuple-element.183, f32[512]{0:T(512)S(1)} %get-tuple-element.182, s32[8192]{0:T(1024)S(1)} %copy-done, s32[512]{0:T(512)S(1)} %bitcast.45), kind=kLoop, calls=%fused_computation.3.clone.1 | loop fusion | flops 20971008 | bytes 16816128 | tf_op jit(solution)/shard_map/while/body/eval_jaxpr/reduce_sum | solution.py:25
  51.7 0.1 dynamic_update_slice.10
  51.8 0.1 dynamic_update_slice.9
  51.9 0.0 copy-start
  51.9 5.1 %fusion.16 = (f32[512]{0:T(512)S(1)}, f32[512,8192]{1,0:T(8,128)S(1)}) fusion(s32[8192]{0:T(1024)} %get-tuple-element.215, s32[512]{0:T(512)S(1)} %bitcast.44, bf16[8192,256]{1,0:T(8,128)(2,1)} %get-tuple-element.217, bf16[6,512,256]{2,1,0:T(8,128)(2,1)} %get-tuple-element.216, s32[]{:T(128)} %get-tuple-element.202), kind=kOutput, calls=%fused_computation.2.clone.1 | convolution fusion | flops 2164260352 | bytes 21271040 | tf_op jit(solution)/shard_map/while/body/eval_jaxpr/dot_general | solution.py:20
  57.1 0.0 copy-done
  57.1 4.6 %fusion.17 = f32[512]{0:T(512)S(1)} fusion(f32[512,8192]{1,0:T(8,128)S(1)} %get-tuple-element.183, f32[512]{0:T(512)S(1)} %get-tuple-element.182, s32[8192]{0:T(1024)S(1)} %copy-done, s32[512]{0:T(512)S(1)} %bitcast.45), kind=kLoop, calls=%fused_computation.3.clone.1 | loop fusion | flops 20971008 | bytes 16816128 | tf_op jit(solution)/shard_map/while/body/eval_jaxpr/reduce_sum | solution.py:25
  61.7 0.1 dynamic_update_slice.10
  61.8 0.1 dynamic_update_slice.9
  61.9 0.0 copy-start
  61.9 5.1 %fusion.16 = (f32[512]{0:T(512)S(1)}, f32[512,8192]{1,0:T(8,128)S(1)}) fusion(s32[8192]{0:T(1024)} %get-tuple-element.215, s32[512]{0:T(512)S(1)} %bitcast.44, bf16[8192,256]{1,0:T(8,128)(2,1)} %get-tuple-element.217, bf16[6,512,256]{2,1,0:T(8,128)(2,1)} %get-tuple-element.216, s32[]{:T(128)} %get-tuple-element.202), kind=kOutput, calls=%fused_computation.2.clone.1 | convolution fusion | flops 2164260352 | bytes 21271040 | tf_op jit(solution)/shard_map/while/body/eval_jaxpr/dot_general | solution.py:20
  67.0 0.0 copy-done
  67.1 4.6 %fusion.17 = f32[512]{0:T(512)S(1)} fusion(f32[512,8192]{1,0:T(8,128)S(1)} %get-tuple-element.183, f32[512]{0:T(512)S(1)} %get-tuple-element.182, s32[8192]{0:T(1024)S(1)} %copy-done, s32[512]{0:T(512)S(1)} %bitcast.45), kind=kLoop, calls=%fused_computation.3.clone.1 | loop fusion | flops 20971008 | bytes 16816128 | tf_op jit(solution)/shard_map/while/body/eval_jaxpr/reduce_sum | solution.py:25
  71.7 0.1 dynamic_update_slice.10
  71.8 0.1 dynamic_update_slice.9
  71.9 0.0 copy-start
  71.9 5.1 %fusion.16 = (f32[512]{0:T(512)S(1)}, f32[512,8192]{1,0:T(8,128)S(1)}) fusion(s32[8192]{0:T(1024)} %get-tuple-element.215, s32[512]{0:T(512)S(1)} %bitcast.44, bf16[8192,256]{1,0:T(8,128)(2,1)} %get-tuple-element.217, bf16[6,512,256]{2,1,0:T(8,128)(2,1)} %get-tuple-element.216, s32[]{:T(128)} %get-tuple-element.202), kind=kOutput, calls=%fused_computation.2.clone.1 | convolution fusion | flops 2164260352 | bytes 21271040 | tf_op jit(solution)/shard_map/while/body/eval_jaxpr/dot_general | solution.py:20
  77.0 0.0 copy-done
  77.0 4.6 %fusion.17 = f32[512]{0:T(512)S(1)} fusion(f32[512,8192]{1,0:T(8,128)S(1)} %get-tuple-element.183, f32[512]{0:T(512)S(1)} %get-tuple-element.182, s32[8192]{0:T(1024)S(1)} %copy-done, s32[512]{0:T(512)S(1)} %bitcast.45), kind=kLoop, calls=%fused_computation.3.clone.1 | loop fusion | flops 20971008 | bytes 16816128 | tf_op jit(solution)/shard_map/while/body/eval_jaxpr/reduce_sum | solution.py:25
  81.7 0.1 dynamic_update_slice.10
  81.8 0.1 dynamic_update_slice.9
  81.8 0.0 copy-start
  81.9 5.1 %fusion.16 = (f32[512]{0:T(512)S(1)}, f32[512,8192]{1,0:T(8,128)S(1)}) fusion(s32[8192]{0:T(1024)} %get-tuple-element.215, s32[512]{0:T(512)S(1)} %bitcast.44, bf16[8192,256]{1,0:T(8,128)(2,1)} %get-tuple-element.217, bf16[6,512,256]{2,1,0:T(8,128)(2,1)} %get-tuple-element.216, s32[]{:T(128)} %get-tuple-element.202), kind=kOutput, calls=%fused_computation.2.clone.1 | convolution fusion | flops 2164260352 | bytes 21271040 | tf_op jit(solution)/shard_map/while/body/eval_jaxpr/dot_general | solution.py:20
  87.0 0.0 copy-done
  87.0 4.6 %fusion.17 = f32[512]{0:T(512)S(1)} fusion(f32[512,8192]{1,0:T(8,128)S(1)} %get-tuple-element.183, f32[512]{0:T(512)S(1)} %get-tuple-element.182, s32[8192]{0:T(1024)S(1)} %copy-done, s32[512]{0:T(512)S(1)} %bitcast.45), kind=kLoop, calls=%fused_computation.3.clone.1 | loop fusion | flops 20971008 | bytes 16816128 | tf_op jit(solution)/shard_map/while/body/eval_jaxpr/reduce_sum | solution.py:25
  91.7 0.1 dynamic_update_slice.10
  91.7 0.1 dynamic_update_slice.9
  91.8 5.2 %all-gather.2 = f32[4,1,3072]{2,1,0:T(1,128)S(1)} all-gather(f32[1,1,3072]{2,1,0:T(1,128)S(1)} %reshape.26), channel_id=1, replica_groups=mesh['dp'=8,'neg'=4] {'neg'}, dimensions={0}, use_global_device_ids=true | all-gather | bytes 61440 | tf_op jit(solution)/shard_map/all_gather | solution.py:11
  97.1 5.2 %all-gather.1 = f32[4,1,3072]{2,1,0:T(1,128)S(1)} all-gather(f32[1,1,3072]{2,1,0:T(1,128)S(1)} %reshape.24), channel_id=1, replica_groups=mesh['dp'=8,'neg'=4] {'neg'}, dimensions={0}, use_global_device_ids=true | all-gather | bytes 61440 | tf_op jit(solution)/shard_map/all_gather | solution.py:11
  102.4 0.2 while.25
  102.6 0.0 copy-done.1
  102.6 2.0 %select_reduce_fusion = (f32[]{:T(128)}, f32[]{:T(128)}, f32[768]{0:T(1024)}) fusion(s32[768]{0:T(1024)S(1)} %copy-done.1, pred[768]{0:T(1024)(128)(4,1)S(1)} %compare_reduce_fusion, s32[]{:T(128)} %bitcast.6, s32[]{:T(128)S(6)} %mul.31, f32[3072]{0:T(1024)S(1)} %get-tuple-element.71, s32[]{:T(128)S(6)} %select_n.15, f32[768]{0:T(1024)S(1)} %multiply_reduce_fusion, ...), kind=kLoop, calls=%fused_computation.16 | loop fusion | flops 13822 | bytes 16148 | tf_op jit(solution)/shard_map/reduce_sum | solution.py:72
  104.6 39.5 %all-reduce = (f32[]{:T(128)}, f32[]{:T(128)}) all-reduce(f32[]{:T(128)} %get-tuple-element.73, f32[]{:T(128)} %get-tuple-element.72), channel_id=1, replica_groups=mesh['dp'=8,'neg'=4] {'dp','neg'}, use_global_device_ids=true, to_apply=%region_9.10 | all-reduce | flops 2 | bytes 16 | tf_op jit(solution)/shard_map/psum | solution.py:72
  (25 shorter events, 0.3 us)
Async XLA Ops:
  7.2 24.8 %all-gather.5.cloned.1.call-start = ((), (), s32[]{:S(2)}) async-start(), calls=%async_computation | async-start | bytes 1966080 | tf_op jit(solution)/shard_map/all_gather | solution.py:46
  31.9 70.7 %copy-start.1 = (s32[768]{0:T(1024)S(1)}, s32[768]{0:T(1024)}, u32[]{:S(2)}) copy-start(s32[768]{0:T(1024)} %param.14) | copy-start | bytes 9220
  31.9 5.2 %copy-start = (s32[8192]{0:T(1024)S(1)}, s32[8192]{0:T(1024)}, u32[]{:S(2)}) copy-start(s32[8192]{0:T(1024)} %get-tuple-element.215) | copy-start | bytes 98308 | tf_op jit(solution)/shard_map/while
  41.9 5.2 %copy-start = (s32[8192]{0:T(1024)S(1)}, s32[8192]{0:T(1024)}, u32[]{:S(2)}) copy-start(s32[8192]{0:T(1024)} %get-tuple-element.215) | copy-start | bytes 98308 | tf_op jit(solution)/shard_map/while
  51.9 5.2 %copy-start = (s32[8192]{0:T(1024)S(1)}, s32[8192]{0:T(1024)}, u32[]{:S(2)}) copy-start(s32[8192]{0:T(1024)} %get-tuple-element.215) | copy-start | bytes 98308 | tf_op jit(solution)/shard_map/while
  61.9 5.2 %copy-start = (s32[8192]{0:T(1024)S(1)}, s32[8192]{0:T(1024)}, u32[]{:S(2)}) copy-start(s32[8192]{0:T(1024)} %get-tuple-element.215) | copy-start | bytes 98308 | tf_op jit(solution)/shard_map/while
  71.9 5.2 %copy-start = (s32[8192]{0:T(1024)S(1)}, s32[8192]{0:T(1024)}, u32[]{:S(2)}) copy-start(s32[8192]{0:T(1024)} %get-tuple-element.215) | copy-start | bytes 98308 | tf_op jit(solution)/shard_map/while
  81.8 5.2 %copy-start = (s32[8192]{0:T(1024)S(1)}, s32[8192]{0:T(1024)}, u32[]{:S(2)}) copy-start(s32[8192]{0:T(1024)} %get-tuple-element.215) | copy-start | bytes 98308 | tf_op jit(solution)/shard_map/while
Sparse Core Ops, SparseCore 0:
  9.5 22.3 all-gather.4
where the time goes:
time: 154 us; the launch traced here: 153 us
  blocking collectives  56.2 us (36%)
  other arithmetic  31.4 us (20%)
  matrix products  30.9 us (20%)
  between operations  16.6 us (11%)
  waiting for transfers between devices  14.4 us (9%)
  local copies, waits for them, and re-layouts  3.64 us (2%)
    psum x1, blocking collectives, shards(): total, count = lax.psum((weighted, jnp.sum(live_weight)), ('dp', 'neg'))  39.5 us
    dot_general x6, matrix products, shard_partials(): lax.dot_general(rows, columns, (((1,), (1,)), ((), ())), preferred_elemen...  30.9 us
    reduce_sum x6, other arithmetic, shard_partials(): jnp.sum(jnp.where(hit, 0.0, jnp.exp(logits - peak[:, None])), axis=1)  27.9 us
    all_gather x1, waiting for transfers between devices, shards(): rows = lax.all_gather(user_embed, 'neg', axis=0, tiled=True)  13.7 us
    all_gather x2, blocking collectives, merged(): pieces = jax.tree.map(lambda part: lax.all_gather(part, axis), value)  10.4 us
    all_gather x1, blocking collectives, shards(): row_ids = lax.all_gather(positive_ids, 'neg', axis=0, tiled=True)  6.2 us
  transfers between devices with their start and end apart: 1, of which 1 were waited for; matrix products, arithmetic and copies ran while one was open for 3% of the time, Pallas kernels for 0%

commit v1 on v0

--- a/solution.py
+++ b/solution.py
@@ -69,7 +69,10 @@
     lse = top + jnp.log(sums * jnp.exp(peaks - top) + jnp.exp(positive - top))
     token_loss = jnp.where(live, lse - positive, 0.0).astype(jnp.float32)
     weighted = jnp.sum(weight * token_loss)
-    total, count = lax.psum((weighted, jnp.sum(live_weight)), ("dp", "neg"))
+    press_points_on = lambda point, link_axis, ax_name: lax.psum(
+        lax.psum(point, axis_name=link_axis), axis_name=ax_name
+    )
+    total, count = press_points_on((weighted, jnp.sum(live_weight)), "dp", "neg")
     return (token_loss, total / count)
 
 

time: 154 us -> 143 us (0.929)
  blocking collectives: 56.2 us -> 45.2 us
    psum x1 -> x2, blocking collectives: 39.5 us -> 28.6 us  [the longest x1 22.1 us: shards(): lax.psum(point, axis_name=link_axis)]
where the time goes in v1:
time: 143 us; the launch traced here: 142 us
  blocking collectives  45.2 us (32%)
  other arithmetic  31.3 us (22%)
  matrix products  30.9 us (22%)
  between operations  16.5 us (12%)
  waiting for transfers between devices  14.4 us (10%)
  local copies, waits for them, and re-layouts  3.64 us (3%)
    dot_general x6, matrix products, shard_partials(): lax.dot_general(rows, columns, (((1,), (1,)), ((), ())), preferred_elemen...  30.9 us
    reduce_sum x6, other arithmetic, shard_partials(): jnp.sum(jnp.where(hit, 0.0, jnp.exp(logits - peak[:, None])), axis=1)  27.9 us
    psum x1, blocking collectives, shards(): lax.psum(point, axis_name=link_axis)  22.1 us
    all_gather x1, waiting for transfers between devices, shards(): rows = lax.all_gather(user_embed, 'neg', axis=0, tiled=True)  13.7 us
    all_gather x2, blocking collectives, merged(): pieces = jax.tree.map(lambda part: lax.all_gather(part, axis), value)  10.4 us
    psum x1, blocking collectives, shards(): lax.psum(lax.psum(point, axis_name=link_axis), axis_name=ax_name)  6.54 us
    all_gather x1, blocking collectives, shards(): row_ids = lax.all_gather(positive_ids, 'neg', axis=0, tiled=True)  6.2 us
  transfers between devices with their start and end apart: 1, of which 1 were waited for; matrix products, arithmetic and copies ran while one was open for 3% of the time, Pallas kernels for 0%

profile of v1, /device:TPU:0, one launch (start us, length us, event | category | flops | bytes accessed | tf_op | source)
XLA Modules:
  0.0 142.4 jit_solution(8937993283505656552)
XLA Ops:
  7.2 0.0 all-gather.5.cloned.1.call-start
  7.2 0.7 all-gather.5.cloned.1.call-update
  7.9 0.7 reshape.22
  8.6 6.2 %all-gather = s32[4,1,768]{2,1,0:T(1,128)S(1)} all-gather(s32[1,1,768]{2,1,0:T(1,128)S(1)} %reshape.22), channel_id=1, replica_groups=mesh['dp'=8,'neg'=4] {'neg'}, dimensions={0}, use_global_device_ids=true | all-gather | bytes 15360 | tf_op jit(solution)/shard_map/all_gather | solution.py:47
  14.9 1.2 slice.18
  16.1 0.7 slice_bitcast_fusion
  16.8 0.1 compare_reduce_fusion
  16.9 1.3 multiply_reduce_fusion
  18.2 13.7 %all-gather.5.cloned.1.call-done = bf16[3072,256]{1,0:T(8,128)(2,1)} async-done(((bf16[768,256]{1,0:T(8,128)(2,1)}), bf16[3072,256]{1,0:T(8,128)(2,1)}) %all-gather.5.cloned.1.call-update) | async-done | bytes 1572880 | tf_op jit(solution)/shard_map/all_gather | solution.py:46
  31.9 0.0 copy-start.1
  31.9 59.9 %while.24 = (s32[]{:T(128)}, f32[6,512]{1,0:T(8,128)S(1)}, f32[6,512]{1,0:T(8,128)S(1)}, s32[6,512]{1,0:T(8,128)S(1)}, s32[8192]{0:T(1024)}, /*index=5*/bf16[6,5...) while((s32[]{:T(128)}, f32[6,512]{1,0:T(8,128)S(1)}, f32[6,512]{1,0:T(8,128)S(1)}, ...), condition=%wide.region_4.5_spmd, body=%wide.region_1.4_spmd.sunk | while | flops 2185231360 | bytes 38230660 | solution.py:56
  31.9 0.0 copy-start
  31.9 5.1 %fusion.16 = (f32[512]{0:T(512)S(1)}, f32[512,8192]{1,0:T(8,128)S(1)}) fusion(s32[8192]{0:T(1024)} %get-tuple-element.217, s32[512]{0:T(512)S(1)} %bitcast.44, bf16[8192,256]{1,0:T(8,128)(2,1)} %get-tuple-element.219, bf16[6,512,256]{2,1,0:T(8,128)(2,1)} %get-tuple-element.218, s32[]{:T(128)} %get-tuple-element.204), kind=kOutput, calls=%fused_computation.2.clone.1 | convolution fusion | flops 2164260352 | bytes 21271040 | tf_op jit(solution)/shard_map/while/body/eval_jaxpr/dot_general | solution.py:20
  37.1 0.0 copy-done
  37.1 4.6 %fusion.17 = f32[512]{0:T(512)S(1)} fusion(f32[512,8192]{1,0:T(8,128)S(1)} %get-tuple-element.185, f32[512]{0:T(512)S(1)} %get-tuple-element.184, s32[8192]{0:T(1024)S(1)} %copy-done, s32[512]{0:T(512)S(1)} %bitcast.45), kind=kLoop, calls=%fused_computation.3.clone.1 | loop fusion | flops 20971008 | bytes 16816128 | tf_op jit(solution)/shard_map/while/body/eval_jaxpr/reduce_sum | solution.py:25
  41.7 0.1 dynamic_update_slice.10
  41.8 0.1 dynamic_update_slice.9
  41.9 0.0 copy-start
  41.9 5.1 %fusion.16 = (f32[512]{0:T(512)S(1)}, f32[512,8192]{1,0:T(8,128)S(1)}) fusion(s32[8192]{0:T(1024)} %get-tuple-element.217, s32[512]{0:T(512)S(1)} %bitcast.44, bf16[8192,256]{1,0:T(8,128)(2,1)} %get-tuple-element.219, bf16[6,512,256]{2,1,0:T(8,128)(2,1)} %get-tuple-element.218, s32[]{:T(128)} %get-tuple-element.204), kind=kOutput, calls=%fused_computation.2.clone.1 | convolution fusion | flops 2164260352 | bytes 21271040 | tf_op jit(solution)/shard_map/while/body/eval_jaxpr/dot_general | solution.py:20
  47.1 0.0 copy-done
  47.1 4.6 %fusion.17 = f32[512]{0:T(512)S(1)} fusion(f32[512,8192]{1,0:T(8,128)S(1)} %get-tuple-element.185, f32[512]{0:T(512)S(1)} %get-tuple-element.184, s32[8192]{0:T(1024)S(1)} %copy-done, s32[512]{0:T(512)S(1)} %bitcast.45), kind=kLoop, calls=%fused_computation.3.clone.1 | loop fusion | flops 20971008 | bytes 16816128 | tf_op jit(solution)/shard_map/while/body/eval_jaxpr/reduce_sum | solution.py:25
  51.7 0.1 dynamic_update_slice.10
  51.8 0.1 dynamic_update_slice.9
  51.9 0.0 copy-start
  51.9 5.1 %fusion.16 = (f32[512]{0:T(512)S(1)}, f32[512,8192]{1,0:T(8,128)S(1)}) fusion(s32[8192]{0:T(1024)} %get-tuple-element.217, s32[512]{0:T(512)S(1)} %bitcast.44, bf16[8192,256]{1,0:T(8,128)(2,1)} %get-tuple-element.219, bf16[6,512,256]{2,1,0:T(8,128)(2,1)} %get-tuple-element.218, s32[]{:T(128)} %get-tuple-element.204), kind=kOutput, calls=%fused_computation.2.clone.1 | convolution fusion | flops 2164260352 | bytes 21271040 | tf_op jit(solution)/shard_map/while/body/eval_jaxpr/dot_general | solution.py:20
  57.1 0.0 copy-done
  57.1 4.6 %fusion.17 = f32[512]{0:T(512)S(1)} fusion(f32[512,8192]{1,0:T(8,128)S(1)} %get-tuple-element.185, f32[512]{0:T(512)S(1)} %get-tuple-element.184, s32[8192]{0:T(1024)S(1)} %copy-done, s32[512]{0:T(512)S(1)} %bitcast.45), kind=kLoop, calls=%fused_computation.3.clone.1 | loop fusion | flops 20971008 | bytes 16816128 | tf_op jit(solution)/shard_map/while/body/eval_jaxpr/reduce_sum | solution.py:25
  61.7 0.1 dynamic_update_slice.10
  61.8 0.1 dynamic_update_slice.9
  61.9 0.0 copy-start
  61.9 5.1 %fusion.16 = (f32[512]{0:T(512)S(1)}, f32[512,8192]{1,0:T(8,128)S(1)}) fusion(s32[8192]{0:T(1024)} %get-tuple-element.217, s32[512]{0:T(512)S(1)} %bitcast.44, bf16[8192,256]{1,0:T(8,128)(2,1)} %get-tuple-element.219, bf16[6,512,256]{2,1,0:T(8,128)(2,1)} %get-tuple-element.218, s32[]{:T(128)} %get-tuple-element.204), kind=kOutput, calls=%fused_computation.2.clone.1 | convolution fusion | flops 2164260352 | bytes 21271040 | tf_op jit(solution)/shard_map/while/body/eval_jaxpr/dot_general | solution.py:20
  67.0 0.0 copy-done
  67.1 4.6 %fusion.17 = f32[512]{0:T(512)S(1)} fusion(f32[512,8192]{1,0:T(8,128)S(1)} %get-tuple-element.185, f32[512]{0:T(512)S(1)} %get-tuple-element.184, s32[8192]{0:T(1024)S(1)} %copy-done, s32[512]{0:T(512)S(1)} %bitcast.45), kind=kLoop, calls=%fused_computation.3.clone.1 | loop fusion | flops 20971008 | bytes 16816128 | tf_op jit(solution)/shard_map/while/body/eval_jaxpr/reduce_sum | solution.py:25
  71.7 0.1 dynamic_update_slice.10
  71.8 0.1 dynamic_update_slice.9
  71.9 0.0 copy-start
  71.9 5.1 %fusion.16 = (f32[512]{0:T(512)S(1)}, f32[512,8192]{1,0:T(8,128)S(1)}) fusion(s32[8192]{0:T(1024)} %get-tuple-element.217, s32[512]{0:T(512)S(1)} %bitcast.44, bf16[8192,256]{1,0:T(8,128)(2,1)} %get-tuple-element.219, bf16[6,512,256]{2,1,0:T(8,128)(2,1)} %get-tuple-element.218, s32[]{:T(128)} %get-tuple-element.204), kind=kOutput, calls=%fused_computation.2.clone.1 | convolution fusion | flops 2164260352 | bytes 21271040 | tf_op jit(solution)/shard_map/while/body/eval_jaxpr/dot_general | solution.py:20
  77.0 0.0 copy-done
  77.0 4.6 %fusion.17 = f32[512]{0:T(512)S(1)} fusion(f32[512,8192]{1,0:T(8,128)S(1)} %get-tuple-element.185, f32[512]{0:T(512)S(1)} %get-tuple-element.184, s32[8192]{0:T(1024)S(1)} %copy-done, s32[512]{0:T(512)S(1)} %bitcast.45), kind=kLoop, calls=%fused_computation.3.clone.1 | loop fusion | flops 20971008 | bytes 16816128 | tf_op jit(solution)/shard_map/while/body/eval_jaxpr/reduce_sum | solution.py:25
  81.7 0.1 dynamic_update_slice.10
  81.8 0.1 dynamic_update_slice.9
  81.8 0.0 copy-start
  81.9 5.1 %fusion.16 = (f32[512]{0:T(512)S(1)}, f32[512,8192]{1,0:T(8,128)S(1)}) fusion(s32[8192]{0:T(1024)} %get-tuple-element.217, s32[512]{0:T(512)S(1)} %bitcast.44, bf16[8192,256]{1,0:T(8,128)(2,1)} %get-tuple-element.219, bf16[6,512,256]{2,1,0:T(8,128)(2,1)} %get-tuple-element.218, s32[]{:T(128)} %get-tuple-element.204), kind=kOutput, calls=%fused_computation.2.clone.1 | convolution fusion | flops 2164260352 | bytes 21271040 | tf_op jit(solution)/shard_map/while/body/eval_jaxpr/dot_general | solution.py:20
  87.0 0.0 copy-done
  87.0 4.6 %fusion.17 = f32[512]{0:T(512)S(1)} fusion(f32[512,8192]{1,0:T(8,128)S(1)} %get-tuple-element.185, f32[512]{0:T(512)S(1)} %get-tuple-element.184, s32[8192]{0:T(1024)S(1)} %copy-done, s32[512]{0:T(512)S(1)} %bitcast.45), kind=kLoop, calls=%fused_computation.3.clone.1 | loop fusion | flops 20971008 | bytes 16816128 | tf_op jit(solution)/shard_map/while/body/eval_jaxpr/reduce_sum | solution.py:25
  91.7 0.1 dynamic_update_slice.10
  91.7 0.1 dynamic_update_slice.9
  91.8 5.2 %all-gather.2 = f32[4,1,3072]{2,1,0:T(1,128)S(1)} all-gather(f32[1,1,3072]{2,1,0:T(1,128)S(1)} %reshape.26), channel_id=1, replica_groups=mesh['dp'=8,'neg'=4] {'neg'}, dimensions={0}, use_global_device_ids=true | all-gather | bytes 61440 | tf_op jit(solution)/shard_map/all_gather | solution.py:11
  97.1 5.2 %all-gather.1 = f32[4,1,3072]{2,1,0:T(1,128)S(1)} all-gather(f32[1,1,3072]{2,1,0:T(1,128)S(1)} %reshape.24), channel_id=1, replica_groups=mesh['dp'=8,'neg'=4] {'neg'}, dimensions={0}, use_global_device_ids=true | all-gather | bytes 61440 | tf_op jit(solution)/shard_map/all_gather | solution.py:11
  102.4 0.2 while.25
  102.6 0.0 copy-done.1
  102.6 2.0 %select_reduce_fusion = (f32[]{:T(128)}, f32[]{:T(128)}, f32[768]{0:T(1024)}) fusion(s32[768]{0:T(1024)S(1)} %copy-done.1, pred[768]{0:T(1024)(128)(4,1)S(1)} %compare_reduce_fusion, s32[]{:T(128)} %bitcast.6, s32[]{:T(128)S(6)} %mul.31, f32[3072]{0:T(1024)S(1)} %get-tuple-element.71, s32[]{:T(128)S(6)} %select_n.15, f32[768]{0:T(1024)S(1)} %multiply_reduce_fusion, ...), kind=kLoop, calls=%fused_computation.16 | loop fusion | flops 13822 | bytes 16148 | tf_op jit(solution)/shard_map/reduce_sum | solution.py:75
  104.6 22.1 %all-reduce = (f32[]{:T(128)}, f32[]{:T(128)}) all-reduce(f32[]{:T(128)} %get-tuple-element.73, f32[]{:T(128)} %get-tuple-element.72), channel_id=1, replica_groups=mesh['dp'=8,'neg'=4] {'dp'}, use_global_device_ids=true, to_apply=%region_9.10 | all-reduce | flops 2 | bytes 16 | tf_op jit(solution)/shard_map/psum | solution.py:73
  126.6 6.5 %all-reduce.1 = (f32[]{:T(128)}, f32[]{:T(128)}) all-reduce(f32[]{:T(128)} %get-tuple-element.98, f32[]{:T(128)} %get-tuple-element.99), channel_id=1, replica_groups=mesh['dp'=8,'neg'=4] {'neg'}, use_global_device_ids=true, to_apply=%region_10.11 | all-reduce | flops 2 | bytes 16 | tf_op jit(solution)/shard_map/psum | solution.py:72
  (25 shorter events, 0.3 us)
Async XLA Ops:
  7.2 24.8 %all-gather.5.cloned.1.call-start = ((), (), s32[]{:S(2)}) async-start(), calls=%async_computation | async-start | bytes 1966080 | tf_op jit(solution)/shard_map/all_gather | solution.py:46
  31.9 70.7 %copy-start.1 = (s32[768]{0:T(1024)S(1)}, s32[768]{0:T(1024)}, u32[]{:S(2)}) copy-start(s32[768]{0:T(1024)} %param.14) | copy-start | bytes 9220
  31.9 5.2 %copy-start = (s32[8192]{0:T(1024)S(1)}, s32[8192]{0:T(1024)}, u32[]{:S(2)}) copy-start(s32[8192]{0:T(1024)} %get-tuple-element.217) | copy-start | bytes 98308 | tf_op jit(solution)/shard_map/while
  41.9 5.2 %copy-start = (s32[8192]{0:T(1024)S(1)}, s32[8192]{0:T(1024)}, u32[]{:S(2)}) copy-start(s32[8192]{0:T(1024)} %get-tuple-element.217) | copy-start | bytes 98308 | tf_op jit(solution)/shard_map/while
  51.9 5.2 %copy-start = (s32[8192]{0:T(1024)S(1)}, s32[8192]{0:T(1024)}, u32[]{:S(2)}) copy-start(s32[8192]{0:T(1024)} %get-tuple-element.217) | copy-start | bytes 98308 | tf_op jit(solution)/shard_map/while
  61.9 5.2 %copy-start = (s32[8192]{0:T(1024)S(1)}, s32[8192]{0:T(1024)}, u32[]{:S(2)}) copy-start(s32[8192]{0:T(1024)} %get-tuple-element.217) | copy-start | bytes 98308 | tf_op jit(solution)/shard_map/while
  71.9 5.2 %copy-start = (s32[8192]{0:T(1024)S(1)}, s32[8192]{0:T(1024)}, u32[]{:S(2)}) copy-start(s32[8192]{0:T(1024)} %get-tuple-element.217) | copy-start | bytes 98308 | tf_op jit(solution)/shard_map/while
  81.8 5.2 %copy-start = (s32[8192]{0:T(1024)S(1)}, s32[8192]{0:T(1024)}, u32[]{:S(2)}) copy-start(s32[8192]{0:T(1024)} %get-tuple-element.217) | copy-start | bytes 98308 | tf_op jit(solution)/shard_map/while
Sparse Core Ops, SparseCore 0:
  9.5 22.3 all-gather.4
